TPU v7x, 32 devices: a whole 2x2x4 slice. The times are simulated.
32 devices in a mesh: replica: 8 (over y, x, core), shard: 4 (over z).
Axes of the slice: x: 2, y: 2, z: 4, core: 2. Of those that a mesh axis runs over, the one named last changes fastest.
Arguments:
- params: float32 [8, 64, 28672], P('replica', 'shard'), may hold values from -6 to 6
- first_moment: float32 [8, 64, 28672], P('replica', 'shard'), may hold values from -3 to 3
- second_moment: float32 [8, 64, 28672], P('replica', 'shard'), may hold values from 0.25 to 4
- grads: bfloat16 [4, 8, 64, 28672], P(None, 'replica', 'shard'), may hold values from -6 to 6
- push_weight: float32 [8], P('replica'), may hold values from 0.5 to 2
Outputs:
- final_weights: bfloat16 [8, 64, 28672], P('replica')
All inputs are finite; a program needn't handle non-finite values.
Results may differ from a plain program's by a relative error of at most 0.001.
Values may be sent and summed in bfloat16 or wider, within the bound.
A program may use at most 64 MiB of HBM per device.

v0:
```python
import functools

import jax
import jax.numpy as jnp
from jax import lax
from jax.experimental import pallas as pl
from jax.experimental.pallas import tpu as pltpu
from jax.sharding import PartitionSpec as P

STEPS = 4


beta_one = 0.9
beta_two = 0.95
learn_rate = 0.1
decay_rate = 0.1
epsilon = 1e-08
adam_offset = 101

CODE_SCALE = 8.0
LAG = 2
HOP_LAG = 2
CHUNKS = 28
LOAD_GROUP = 4
GATHER_GROUP = 1
MESH = pl.DeviceIdType.MESH


def plan_of(replicas):
    levels = replicas.bit_length() - 1
    distances = [2 ** (step % levels) for step in range(STEPS)]
    every = {2**level for level in range(levels)}
    plan = []
    for step, distance in enumerate(distances):
        later = set(distances[step + 1 :])
        if every <= later:
            continue
        above = {d for d in every if d > distance}
        plan.append((step, distance, above <= later))
    return plan


def encode(value):
    power = value * CODE_SCALE
    power = power * power
    power = power * power
    power = power * power
    power = power * power
    return jnp.where(value < 0.0, -power, power).astype(jnp.bfloat16)


def decode(code):
    code = code.astype(jnp.float32)
    size = jnp.exp(jnp.log(jnp.abs(code)) * (1.0 / 16.0)) * (1.0 / CODE_SCALE)
    return jnp.where(code < 0.0, -size, size)


def kernel(
    plan, replicas, shards, chunks, chunk, sub, load_group, gather_group,
    params_ref, first_ref, second_ref, grads_ref, weight_ref, out_ref,
    params, first, second, grads, weights, scales, acc, terms, sent, arrived, final,
    load_sem, wsend, wrecv, xsend, xrecv, zsend, zrecv, own_sem,
):
    me, z = lax.axis_index("replica"), lax.axis_index("shard")
    rows = params.shape[0]
    rounds = len(plan)
    keep = 1.0 - learn_rate * decay_rate

    def columns(i, group=1):
        return pl.ds(pl.multiple_of(i * (group * chunk), chunk), group * chunk)

    def slab(index):
        return pl.ds(pl.multiple_of(index * rows, rows), rows)

    def peer(offset):
        return lax.rem(me + offset + replicas, replicas)

    barrier = pltpu.get_barrier_semaphore()
    for k in range(1, replicas):
        pl.semaphore_signal(barrier, inc=1, device_id={"replica": peer(k)}, device_id_type=MESH)

    @pl.when(z > 0)
    def _():
        pl.semaphore_signal(barrier, inc=1, device_id={"shard": z - 1}, device_id_type=MESH)

    @pl.when(z < shards - 1)
    def _():
        pl.semaphore_signal(barrier, inc=1, device_id={"shard": z + 1}, device_id_type=MESH)

    def loads(i):
        cols = columns(i, load_group)
        return (
            pltpu.make_async_copy(params_ref.at[0, :, cols], params.at[:, cols], load_sem.at[0, i]),
            pltpu.make_async_copy(first_ref.at[0, :, cols], first.at[:, cols], load_sem.at[1, i]),
            pltpu.make_async_copy(second_ref.at[0, :, cols], second.at[:, cols], load_sem.at[2, i]),
            pltpu.make_async_copy(grads_ref.at[:, 0, :, cols], grads.at[:, :, cols], load_sem.at[3, i]),
        )

    @pl.loop(0, chunks // load_group)
    def _(i):
        for copy in loads(i):
            copy.start()

    weights[me] = jnp.full(weights.shape[1:], weight_ref[0], jnp.float32)
    ends_of_line = jnp.where(z > 0, 1, 0) + jnp.where(z < shards - 1, 1, 0)
    pl.semaphore_wait(barrier, replicas - 1 + ends_of_line)

    def weight_copy(k, owner):
        return pltpu.make_async_remote_copy(
            src_ref=weights.at[owner], dst_ref=weights.at[owner],
            send_sem=wsend.at[k - 1], recv_sem=wrecv.at[k - 1],
            device_id={"replica": peer(k)}, device_id_type=MESH,
        )

    for k in range(1, replicas):
        weight_copy(k, me).start()
    for k in range(1, replicas):
        weight_copy(k, peer(-k)).wait_recv()

    def wide(tile):
        tile = jnp.concatenate([tile] * (rows // tile.shape[0]), axis=0) if rows > tile.shape[0] else tile[:rows]
        return jnp.concatenate([tile] * (sub // tile.shape[1]), axis=1)

    levels = replicas.bit_length() - 1
    behind = [weights[peer(-k)] for k in range(replicas)]
    ends = [step for step, _, _ in plan]
    for step in range(STEPS):
        end = min(e for e in ends if e >= step)
        if step == 0:
            scales[0] = wide(behind[0] * keep ** (end + 1))
        scales[1 + step] = wide(behind[0] * (learn_rate * keep ** (end - step)))
        distance = 2 ** (step % levels)
        behind = [0.5 * behind[k] + 0.5 * behind[(k + distance) % replicas] for k in range(replicas)]
    scales[1 + STEPS] = wide(0.5 / behind[0])

    def exchange(k, i):
        _, distance, swap = plan[k]
        if swap:
            to = me + distance - 2 * distance * lax.rem(me // distance, 2)
        else:
            to = peer(distance)
        cols = slice(None) if i is None else columns(i)
        return pltpu.make_async_remote_copy(
            src_ref=sent.at[k, :, cols], dst_ref=arrived.at[k, :, cols],
            send_sem=xsend.at[k], recv_sem=xrecv.at[k, 0 if i is None else i],
            device_id={"replica": to}, device_id_type=MESH,
        )

    def gather(way, hop, i):
        sign = 1 - 2 * way
        cols, index = slice(None) if i is None else columns(i, gather_group), z - sign * hop
        target = out_ref.at[0, slab(index), cols]
        return pltpu.make_async_remote_copy(
            src_ref=final.at[:, cols] if hop == 0 else target, dst_ref=target,
            send_sem=zsend.at[way, hop], recv_sem=zrecv.at[way, hop, 0 if i is None else i],
            device_id={"shard": z + sign}, device_id_type=MESH,
        )

    def gathered(way, hop, i):
        sign = 1 - 2 * way
        target = out_ref.at[0, slab(z - sign * hop), columns(i, gather_group)]
        return pltpu.make_async_remote_copy(
            src_ref=target, dst_ref=target,
            send_sem=zsend.at[way, hop - 1], recv_sem=zrecv.at[way, hop - 1, i],
            device_id={"shard": z - sign}, device_id_type=MESH,
        )

    def has_source(way, hop):
        return z >= hop if way == 0 else z + hop < shards

    def has_target(way):
        return z < shards - 1 if way == 0 else z > 0

    def own(i):
        cols = slice(None) if i is None else columns(i, gather_group)
        return pltpu.make_async_copy(final.at[:, cols], out_ref.at[0, slab(z), cols], own_sem)

    def start_round(i):
        @pl.when(lax.rem(i, load_group) == 0)
        def _():
            for copy in loads(i // load_group):
                copy.wait()

        for j in range(chunk // sub):
            cols = pl.ds(pl.multiple_of(i * chunk + j * sub, sub), sub)
            m, v = first[:, cols], second[:, cols]
            total = scales[0] * params[:, cols]
            k = 0
            for step in range(STEPS):
                g = grads[step, :, cols].astype(jnp.float32)
                count = adam_offset + step
                m = beta_one * m + (1.0 - beta_one) * g
                v = beta_two * v + (1.0 - beta_two) * g * g
                fixed = jnp.sqrt(v * (1.0 / (1.0 - beta_two**count))) + epsilon
                update = m * (1.0 / (1.0 - beta_one**count)) / fixed * scales[1 + step]
                total = -update if total is None else total - update
                if step == ends[k]:
                    if k == 0:
                        acc[:, cols] = total
                        sent[0, :, cols] = encode(total)
                    else:
                        terms[k - 1, :, cols] = total
                    total, k = None, k + 1
        exchange(0, i).start()

    def next_round(k, i):
        exchange(k - 1, i).wait_recv()
        for j in range(chunk // sub):
            cols = pl.ds(pl.multiple_of(i * chunk + j * sub, sub), sub)
            both = acc[:, cols] + decode(arrived[k - 1, :, cols])
            if k < rounds:
                both = both * (0.5 * keep ** (ends[k] - ends[k - 1])) + terms[k - 1, :, cols]
                acc[:, cols] = both
                sent[k, :, cols] = encode(both)
            else:
                final[:, cols] = (both * scales[1 + STEPS]).astype(jnp.bfloat16)
        if k < rounds:
            exchange(k, i).start()
        else:

            @pl.when(lax.rem(i, gather_group) == gather_group - 1)
            def _():
                for way in range(2):
                    pl.when(has_target(way))(lambda way=way: gather(way, 0, i // gather_group).start())
                own(i // gather_group).start()

    def pass_on(hop, i):
        for way in range(2):

            whole = lax.rem(i, gather_group) == gather_group - 1

            @pl.when(jnp.logical_and(whole, jnp.logical_and(has_target(way), has_source(way, hop))))
            def _(way=way):
                gathered(way, hop, i // gather_group).wait_recv()
                gather(way, hop, i // gather_group).start()

    hops = shards - 2

    @pl.loop(0, chunks + rounds * LAG + max(hops, 0) * HOP_LAG)
    def _(t):
        def at(delay, act):
            i = t - delay

            @pl.when(jnp.logical_and(i >= 0, i < chunks))
            def _():
                act(i)

        at(0, start_round)
        for k in range(1, rounds + 1):
            at(k * LAG, functools.partial(next_round, k))
        for hop in range(1, hops + 1):
            at(rounds * LAG + hop * HOP_LAG, functools.partial(pass_on, hop))

    for way in range(2):

        @pl.when(jnp.logical_not(has_target(way)))
        def _(way=way):
            @pl.loop(0, chunks // gather_group)
            def _(i):
                for hop in range(1, shards):
                    pl.when(has_source(way, hop))(lambda hop=hop: gathered(way, hop, i).wait_recv())

    for k in range(1, replicas):
        weight_copy(k, me).wait_send()
    for k in range(rounds):
        exchange(k, None).wait_send()
    own(None).wait()
    for way in range(2):
        for hop in range(shards - 1):

            @pl.when(jnp.logical_and(has_target(way), has_source(way, hop)))
            def _(way=way, hop=hop):
                gather(way, hop, None).wait_send()


def per_device(params, first_moment, second_moment, grads, push_weight):
    replicas, shards = lax.axis_size("replica"), lax.axis_size("shard")
    _, rows, cols = params.shape
    units = cols // 128
    chunks = max(n for n in range(1, CHUNKS + 1) if units % n == 0)
    chunk = cols // chunks
    sub = max(128 * n for n in (1, 2) if chunk % (128 * n) == 0)
    load_group = LOAD_GROUP if chunks % LOAD_GROUP == 0 else 1
    gather_group = GATHER_GROUP if chunks % GATHER_GROUP == 0 else 1
    plan = plan_of(replicas)
    rounds = len(plan)
    f32, bf16, dma = jnp.float32, jnp.bfloat16, pltpu.SemaphoreType.DMA
    anywhere = pl.BlockSpec(memory_space=pl.ANY)
    body = functools.partial(kernel, plan, replicas, shards, chunks, chunk, sub, load_group, gather_group)
    hops = max(shards - 1, 1)
    large = (params, first_moment, second_moment, grads)
    large = tuple(pltpu.with_memory_space_constraint(x, pltpu.HBM) for x in large)
    return pl.pallas_call(
        body,
        out_shape=jax.ShapeDtypeStruct((1, rows * shards, cols), bf16),
        in_specs=[anywhere] * 4 + [pl.BlockSpec(memory_space=pltpu.SMEM)],
        out_specs=anywhere,
        scratch_shapes=[
            pltpu.VMEM((rows, cols), f32),
            pltpu.VMEM((rows, cols), f32),
            pltpu.VMEM((rows, cols), f32),
            pltpu.VMEM((STEPS, rows, cols), bf16),
            pltpu.VMEM((replicas, 8, 128), f32),
            pltpu.VMEM((STEPS + 2, rows, sub), f32),
            pltpu.VMEM((rows, cols), f32),
            pltpu.VMEM((max(rounds - 1, 1), rows, cols), f32),
            pltpu.VMEM((rounds, rows, cols), bf16),
            pltpu.VMEM((rounds, rows, cols), bf16),
            pltpu.VMEM((rows, cols), bf16),
            dma((4, chunks // load_group)),
            dma((replicas - 1,)),
            dma((replicas - 1,)),
            dma((rounds,)),
            dma((rounds, chunks)),
            dma((2, hops)),
            dma((2, hops, chunks // gather_group)),
            dma,
        ],
        compiler_params=pltpu.CompilerParams(
            collective_id=0, has_side_effects=True, vmem_limit_bytes=48 * 1024 * 1024
        ),
    )(*large, push_weight)


def solution(mesh):
    return jax.shard_map(
        per_device,
        mesh=mesh,
        in_specs=(
            P("replica", "shard", None),
            P("replica", "shard", None),
            P("replica", "shard", None),
            P(None, "replica", "shard", None),
            P("replica"),
        ),
        out_specs=P("replica", None, None),
        check_vma=False,
    )
```

profile of v0, /device:TPU:0, one launch (start us, length us, event | category | flops | bytes accessed | tf_op | source)
XLA Modules:
  0.0 83.6 jit_solution(16417286641781498905)
XLA Ops:
  0.7 81.1 %shard_map.55 = bf16[1,64,28672]{2,1,0:T(8,128)(2,1)S(1)} custom-call(f32[1,16,28672]{2,1,0:T(8,128)} %params_ref.1, f32[1,16,28672]{2,1,0:T(8,128)} %first_ref.1, f32[1,16,28672]{2,1,0:T(8,128)} %second_ref.1, bf16[4,1,16,28672]{3,2,1,0:T(8,128)(2,1)} %grads_ref.1, f32[1]{0:T(128)S(6)} %copy.7.weight_ref), custom_call_target="tpu_custom_call" | custom-call | tf_op jit(solution)/shard_map/pallas_call | solution.py:293
  81.8 1.8 %copy.8 = bf16[1,64,28672]{2,1,0:T(8,128)(2,1)} copy(bf16[1,64,28672]{2,1,0:T(8,128)(2,1)S(1)} %shard_map.55) | data formatting | bytes 7340032
where the time goes:
time: 83.8 us; the launch traced here: 83.6 us
  Pallas kernels  81.1 us (97%)
  local copies, waits for them, and re-layouts  1.84 us (2%)
    pallas_call x1, Pallas kernels, per_device(): pl.pallas_call(body, out_shape=jax.ShapeDtypeStruct((1, rows * shards, co...  81.1 us
    unnamed x1, local copies, waits for them, and re-layouts  1.84 us

commit v1 on v0

v1 whole, which is shorter than its diff:
```python
import functools

import jax
import jax.numpy as jnp
from jax import lax
from jax.experimental import pallas as pl
from jax.experimental.pallas import tpu as pltpu
from jax.sharding import PartitionSpec as P

STEPS = 4


beta_one = 0.9
beta_two = 0.95
learn_rate = 0.1
decay_rate = 0.1
epsilon = 1e-08
adam_offset = 101

CODE_SCALE = 8.0
LAG = 3
HOP_LAG = 2
CHUNKS = 28
PARTS = 1
EARLY = 2
LOAD_GROUP = 2
SUB = 2
MESH = pl.DeviceIdType.MESH


def plan_of(replicas):
    levels = replicas.bit_length() - 1
    distances = [2 ** (step % levels) for step in range(STEPS)]
    every = {2**level for level in range(levels)}
    plan = []
    for step, distance in enumerate(distances):
        later = set(distances[step + 1 :])
        if every <= later:
            continue
        above = {d for d in every if d > distance}
        plan.append((step, distance, above <= later))
    return plan


def mixes_of(replicas):
    levels = replicas.bit_length() - 1
    mixes = [{0: 1.0}]
    for step in range(STEPS):
        distance, mixed = 2 ** (step % levels), {}
        for k, share in mixes[-1].items():
            for back in (k, (k + distance) % replicas):
                mixed[back] = mixed.get(back, 0.0) + 0.5 * share
        mixes.append(mixed)
    return mixes


def encode(value):
    power = value * CODE_SCALE
    power = power * power
    power = power * power
    power = power * power
    power = power * power
    return jnp.where(value < 0.0, -power, power).astype(jnp.bfloat16)


def decode(code):
    code = code.astype(jnp.float32)
    size = jnp.exp(jnp.log(jnp.abs(code)) * (1.0 / 16.0)) * (1.0 / CODE_SCALE)
    return jnp.where(code < 0.0, -size, size)


def kernel(
    plan, mixes, replicas, shards, chunks, chunk, parts, sub, load_group,
    params_ref, first_ref, second_ref, grads_ref, weight_ref, out_ref,
    params, first, second, grads, weights, scales, acc, terms, early, sent, arrived, final,
    load_sem, wsend, wrecv, xsend, xrecv, zsend, zrecv, own_sem,
):
    me, z = lax.axis_index("replica"), lax.axis_index("shard")
    rows = params.shape[0]
    rounds = len(plan)
    ends = [step for step, _, _ in plan]
    keep = 1.0 - learn_rate * decay_rate
    width = chunk // parts
    small = [(p * width, width, p) for p in range(parts)]

    def whole(i):
        return pl.multiple_of(i * chunk, chunk), chunk, i + parts - 1

    def columns(piece):
        return pl.ds(piece[0], piece[1])

    def slab(index):
        return pl.ds(pl.multiple_of(index * rows, rows), rows)

    def peer(offset):
        return lax.rem(me + offset + replicas, replicas)

    barrier = pltpu.get_barrier_semaphore()
    for k in range(1, replicas):
        pl.semaphore_signal(barrier, inc=1, device_id={"replica": peer(k)}, device_id_type=MESH)

    @pl.when(z > 0)
    def _():
        pl.semaphore_signal(barrier, inc=1, device_id={"shard": z - 1}, device_id_type=MESH)

    @pl.when(z < shards - 1)
    def _():
        pl.semaphore_signal(barrier, inc=1, device_id={"shard": z + 1}, device_id_type=MESH)

    def loads(g):
        cols = pl.ds(pl.multiple_of(g * (load_group * chunk), chunk), load_group * chunk)
        return (
            pltpu.make_async_copy(params_ref.at[0, :, cols], params.at[:, cols], load_sem.at[0, g]),
            pltpu.make_async_copy(first_ref.at[0, :, cols], first.at[:, cols], load_sem.at[1, g]),
            pltpu.make_async_copy(second_ref.at[0, :, cols], second.at[:, cols], load_sem.at[2, g]),
            pltpu.make_async_copy(grads_ref.at[:, 0, :, cols], grads.at[:, :, cols], load_sem.at[3, g]),
        )

    @pl.loop(0, chunks // load_group)
    def _(g):
        for copy in loads(g):
            copy.start()

    weights[me] = jnp.full(weights.shape[1:], weight_ref[0], jnp.float32)
    ends_of_line = jnp.where(z > 0, 1, 0) + jnp.where(z < shards - 1, 1, 0)
    pl.semaphore_wait(barrier, replicas - 1 + ends_of_line)

    def weight_copy(k, owner):
        return pltpu.make_async_remote_copy(
            src_ref=weights.at[owner], dst_ref=weights.at[owner],
            send_sem=wsend.at[k - 1], recv_sem=wrecv.at[k - 1],
            device_id={"replica": peer(k)}, device_id_type=MESH,
        )

    for k in range(1, replicas):
        weight_copy(k, me).start()

    def wide(tile):
        tile = jnp.concatenate([tile] * (rows // tile.shape[0]), axis=0) if rows > tile.shape[0] else tile[:rows]
        return jnp.concatenate([tile] * (sub // tile.shape[1]), axis=1)

    heard = set()

    def mixed(level):
        total = None
        for k, share in sorted(mixes[level].items()):
            if k and k not in heard:
                weight_copy(k, peer(-k)).wait_recv()
                heard.add(k)
            part = share * weights[peer(-k)]
            total = part if total is None else total + part
        return total

    def scale_of(step):
        end = min(e for e in ends if e >= step)
        scales[1 + step] = wide(mixed(step) * (learn_rate * keep ** (end - step)))

    def exchange(k, piece):
        _, distance, swap = plan[k]
        if swap:
            to = me + distance - 2 * distance * lax.rem(me // distance, 2)
        else:
            to = peer(distance)
        cols = slice(None) if piece is None else columns(piece)
        return pltpu.make_async_remote_copy(
            src_ref=sent.at[k, :, cols], dst_ref=arrived.at[k, :, cols],
            send_sem=xsend.at[k], recv_sem=xrecv.at[k, 0 if piece is None else piece[2]],
            device_id={"replica": to}, device_id_type=MESH,
        )

    def gather(way, hop, piece):
        sign = 1 - 2 * way
        cols, index = slice(None) if piece is None else columns(piece), z - sign * hop
        target = out_ref.at[0, slab(index), cols]
        return pltpu.make_async_remote_copy(
            src_ref=final.at[:, cols] if hop == 0 else target, dst_ref=target,
            send_sem=zsend.at[way, hop], recv_sem=zrecv.at[way, hop, 0 if piece is None else piece[2]],
            device_id={"shard": z + sign}, device_id_type=MESH,
        )

    def gathered(way, hop, piece):
        sign = 1 - 2 * way
        target = out_ref.at[0, slab(z - sign * hop), columns(piece)]
        return pltpu.make_async_remote_copy(
            src_ref=target, dst_ref=target,
            send_sem=zsend.at[way, hop - 1], recv_sem=zrecv.at[way, hop - 1, piece[2]],
            device_id={"shard": z - sign}, device_id_type=MESH,
        )

    def has_source(way, hop):
        return z >= hop if way == 0 else z + hop < shards

    def has_target(way):
        return z < shards - 1 if way == 0 else z > 0

    def own(piece):
        cols = slice(None) if piece is None else columns(piece)
        return pltpu.make_async_copy(final.at[:, cols], out_ref.at[0, slab(z), cols], own_sem)

    def adam(cols, known):
        m, v = first[:, cols], second[:, cols]
        total = scales[0] * params[:, cols]
        for step in range(STEPS):
            g = grads[step, :, cols].astype(jnp.float32)
            count = adam_offset + step
            m = beta_one * m + (1.0 - beta_one) * g
            v = beta_two * v + (1.0 - beta_two) * g * g
            fixed = jnp.sqrt(v * (1.0 / (1.0 - beta_two**count))) + epsilon
            update = m * (1.0 / (1.0 - beta_one**count)) / fixed
            if step > ends[0]:
                terms[step - ends[0] - 1, :, cols] = update
            elif step < known:
                total = total - update * scales[1 + step]
            else:
                early[step - known, :, cols] = update
        return total

    def tiles(piece):
        for j in range(piece[1] // sub):
            yield pl.ds(pl.multiple_of(piece[0] + j * sub, sub), sub)

    def first_half(piece):
        for cols in tiles(piece):
            acc[:, cols] = adam(cols, 1)

    def second_half(piece):
        for cols in tiles(piece):
            total = acc[:, cols]
            for step in range(1, ends[0] + 1):
                total = total - early[step - 1, :, cols] * scales[1 + step]
            acc[:, cols] = total
            sent[0, :, cols] = encode(total)
        exchange(0, piece).start()

    def start_round(piece):
        for cols in tiles(piece):
            total = adam(cols, STEPS)
            acc[:, cols] = total
            sent[0, :, cols] = encode(total)
        exchange(0, piece).start()

    def next_round(k, piece):
        exchange(k - 1, piece).wait_recv()
        for cols in tiles(piece):
            both = acc[:, cols] + decode(arrived[k - 1, :, cols])
            if k < rounds:
                both = both * (0.5 * keep ** (ends[k] - ends[k - 1])) - terms[k - 1, :, cols] * scales[1 + ends[k]]
                acc[:, cols] = both
                sent[k, :, cols] = encode(both)
            else:
                final[:, cols] = (both * scales[1 + STEPS]).astype(jnp.bfloat16)
        if k < rounds:
            exchange(k, piece).start()
        else:
            for way in range(2):
                pl.when(has_target(way))(lambda way=way: gather(way, 0, piece).start())
            own(piece).start()

    def pass_on(hop, piece):
        for way in range(2):

            @pl.when(jnp.logical_and(has_target(way), has_source(way, hop)))
            def _(way=way):
                gathered(way, hop, piece).wait_recv()
                gather(way, hop, piece).start()

    def wait_loads(i):
        @pl.when(lax.rem(i, load_group) == 0)
        def _():
            for copy in loads(i // load_group):
                copy.wait()

    scales[0] = wide(mixed(0) * keep ** (ends[0] + 1))
    scale_of(0)
    for i in range(EARLY):
        if i % load_group == 0:
            for copy in loads(i // load_group):
                copy.wait()
        for piece in small if i == 0 else [whole(i)]:
            first_half(piece)
    for step in range(1, ends[0] + 1):
        scale_of(step)
    for i in range(EARLY):
        for piece in small if i == 0 else [whole(i)]:
            second_half(piece)
    wait_loads(EARLY)
    start_round(whole(EARLY))
    for step in range(ends[0] + 1, STEPS):
        scale_of(step)
    scales[1 + STEPS] = wide(0.5 / mixed(STEPS))

    hops = max(shards - 2, 0)
    last = rounds * LAG

    @pl.loop(EARLY + 1, chunks + last + hops * HOP_LAG)
    def _(t):
        def at(delay, act, low=0):
            i = t - delay
            if low == 0 and parts > 1:

                @pl.when(i == 0)
                def _():
                    for piece in small:
                        act(piece)

                low = 1

            @pl.when(jnp.logical_and(i >= low, i < chunks))
            def _():
                act(whole(i))

        @pl.when(t < chunks)
        def _():
            wait_loads(t)
            start_round(whole(t))

        for k in range(1, rounds + 1):
            at(k * LAG, functools.partial(next_round, k))
        for hop in range(1, hops + 1):
            at(last + hop * HOP_LAG, functools.partial(pass_on, hop))

    for way in range(2):

        @pl.when(jnp.logical_not(has_target(way)))
        def _(way=way):
            def drain(piece):
                for hop in range(1, shards):
                    pl.when(has_source(way, hop))(lambda hop=hop: gathered(way, hop, piece).wait_recv())

            for piece in small:
                drain(piece)

            @pl.loop(1, chunks)
            def _(i):
                drain(whole(i))

    for k in range(1, replicas):
        weight_copy(k, me).wait_send()
    for k in range(rounds):
        exchange(k, None).wait_send()
    own(None).wait()
    for way in range(2):
        for hop in range(shards - 1):

            @pl.when(jnp.logical_and(has_target(way), has_source(way, hop)))
            def _(way=way, hop=hop):
                gather(way, hop, None).wait_send()


def per_device(params, first_moment, second_moment, grads, push_weight):
    replicas, shards = lax.axis_size("replica"), lax.axis_size("shard")
    _, rows, cols = params.shape
    units = cols // 128
    chunks = max(n for n in range(1, CHUNKS + 1) if units % n == 0)
    chunk = cols // chunks
    parts = PARTS if chunk % (128 * PARTS) == 0 else 1
    sub = max(128 * n for n in range(1, SUB + 1) if (chunk // parts) % (128 * n) == 0)
    load_group = LOAD_GROUP if chunks % LOAD_GROUP == 0 else 1
    plan, mixes = plan_of(replicas), mixes_of(replicas)
    rounds = len(plan)
    pieces = chunks + parts - 1
    f32, bf16, dma = jnp.float32, jnp.bfloat16, pltpu.SemaphoreType.DMA
    anywhere = pl.BlockSpec(memory_space=pl.ANY)
    body = functools.partial(kernel, plan, mixes, replicas, shards, chunks, chunk, parts, sub, load_group)
    hops = max(shards - 1, 1)
    large = (params, first_moment, second_moment, grads)
    large = tuple(pltpu.with_memory_space_constraint(x, pltpu.HBM) for x in large)
    return pl.pallas_call(
        body,
        out_shape=jax.ShapeDtypeStruct((1, rows * shards, cols), bf16),
        in_specs=[anywhere] * 4 + [pl.BlockSpec(memory_space=pltpu.SMEM)],
        out_specs=anywhere,
        scratch_shapes=[
            pltpu.VMEM((rows, cols), f32),
            pltpu.VMEM((rows, cols), f32),
            pltpu.VMEM((rows, cols), f32),
            pltpu.VMEM((STEPS, rows, cols), bf16),
            pltpu.VMEM((replicas, 8, 128), f32),
            pltpu.VMEM((STEPS + 2, rows, sub), f32),
            pltpu.VMEM((rows, cols), f32),
            pltpu.VMEM((max(rounds - 1, 1), rows, cols), f32),
            pltpu.VMEM((max(plan[0][0], 1), rows, EARLY * chunk), f32),
            pltpu.VMEM((rounds, rows, cols), bf16),
            pltpu.VMEM((rounds, rows, cols), bf16),
            pltpu.VMEM((rows, cols), bf16),
            dma((4, chunks // load_group)),
            dma((replicas - 1,)),
            dma((replicas - 1,)),
            dma((rounds,)),
            dma((rounds, pieces)),
            dma((2, hops)),
            dma((2, hops, pieces)),
            dma,
        ],
        compiler_params=pltpu.CompilerParams(
            collective_id=0, has_side_effects=True, vmem_limit_bytes=48 * 1024 * 1024
        ),
    )(*large, push_weight)


def solution(mesh):
    return jax.shard_map(
        per_device,
        mesh=mesh,
        in_specs=(
            P("replica", "shard", None),
            P("replica", "shard", None),
            P("replica", "shard", None),
            P(None, "replica", "shard", None),
            P("replica"),
        ),
        out_specs=P("replica", None, None),
        check_vma=False,
    )
```

time: 83.8 us -> 81.8 us (0.976)
  Pallas kernels: 81.1 us -> 79.2 us
    pallas_call x1, Pallas kernels: 81.1 us -> 79.2 us  [per_device(): pl.pallas_call(body, out_shape=jax.ShapeDtypeStruct((1, rows * shards, co...]
where the time goes in v1:
time: 81.8 us; the launch traced here: 81.7 us
  Pallas kernels  79.2 us (97%)
  local copies, waits for them, and re-layouts  1.84 us (2%)
    pallas_call x1, Pallas kernels, per_device(): pl.pallas_call(body, out_shape=jax.ShapeDtypeStruct((1, rows * shards, co...  79.2 us
    unnamed x1, local copies, waits for them, and re-layouts  1.84 us

profile of v1, /device:TPU:0, one launch (start us, length us, event | category | flops | bytes accessed | tf_op | source)
XLA Modules:
  0.0 81.7 jit_solution(11474487297612439270)
XLA Ops:
  0.7 79.2 %shard_map.55 = bf16[1,64,28672]{2,1,0:T(8,128)(2,1)S(1)} custom-call(f32[1,16,28672]{2,1,0:T(8,128)} %params_ref.1, f32[1,16,28672]{2,1,0:T(8,128)} %first_ref.1, f32[1,16,28672]{2,1,0:T(8,128)} %second_ref.1, bf16[4,1,16,28672]{3,2,1,0:T(8,128)(2,1)} %grads_ref.1, f32[1]{0:T(128)S(6)} %copy.7.weight_ref), custom_call_target="tpu_custom_call" | custom-call | tf_op jit(solution)/shard_map/pallas_call | solution.py:368
  79.8 1.8 %copy.8 = bf16[1,64,28672]{2,1,0:T(8,128)(2,1)} copy(bf16[1,64,28672]{2,1,0:T(8,128)(2,1)S(1)} %shard_map.55) | data formatting | bytes 7340032

commit v2 on v1

--- a/solution.py
+++ b/solution.py
@@ -18,10 +18,13 @@
 adam_offset = 101
 
 CODE_SCALE = 8.0
+GAP_SCALE = 16.0
 LAG = 3
 HOP_LAG = 2
 CHUNKS = 28
-PARTS = 1
+OPEN_LAG = 18
+FOLD_LAG = 2
+FULL_TAIL = 3
 EARLY = 2
 LOAD_GROUP = 2
 SUB = 2
@@ -54,8 +57,8 @@
     return mixes
 
 
-def encode(value):
-    power = value * CODE_SCALE
+def encode(value, scale=CODE_SCALE):
+    power = value * scale
     power = power * power
     power = power * power
     power = power * power
@@ -63,31 +66,52 @@
     return jnp.where(value < 0.0, -power, power).astype(jnp.bfloat16)
 
 
-def decode(code):
+def decode(code, scale=CODE_SCALE):
     code = code.astype(jnp.float32)
-    size = jnp.exp(jnp.log(jnp.abs(code)) * (1.0 / 16.0)) * (1.0 / CODE_SCALE)
+    size = jnp.exp(jnp.log(jnp.abs(code)) * (1.0 / 16.0)) * (1.0 / scale)
     return jnp.where(code < 0.0, -size, size)
 
 
 def kernel(
-    plan, mixes, replicas, shards, chunks, chunk, parts, sub, load_group,
+    plan, mixes, replicas, shards, chunks, chunk, sub, load_group, spares,
     params_ref, first_ref, second_ref, grads_ref, weight_ref, out_ref,
     params, first, second, grads, weights, scales, acc, terms, early, sent, arrived, final,
-    load_sem, wsend, wrecv, xsend, xrecv, zsend, zrecv, own_sem,
+    load_sem, wsend, wrecv, xsend, xrecv, zsend, zrecv,
+    codes=None, extra=None, hold=None, gap=None, gaps=None,
+    rsend=None, rrecv=None, gsend=None, grecv=None,
 ):
     me, z = lax.axis_index("replica"), lax.axis_index("shard")
     rows = params.shape[0]
     rounds = len(plan)
     ends = [step for step, _, _ in plan]
     keep = 1.0 - learn_rate * decay_rate
-    width = chunk // parts
-    small = [(p * width, width, p) for p in range(parts)]
-
-    def whole(i):
-        return pl.multiple_of(i * chunk, chunk), chunk, i + parts - 1
-
-    def columns(piece):
-        return pl.ds(piece[0], piece[1])
+    coded = spares > 0
+    side, column, line = lax.rem(me, 2), lax.rem(me // 2, 2), me // 4
+    foreign = shards - 1
+
+    def columns(i):
+        return pl.ds(pl.multiple_of(i * chunk, chunk), chunk)
+
+    def spread(count):
+        return pl.ds(0, count * chunk)
+
+    def at_end(z):
+        return jnp.logical_or(z == 0, z == shards - 1)
+
+    def spared(i):
+        return jnp.logical_and(i >= 1, i <= 4 * spares)
+
+    def same_column(i):
+        return lax.rem(i, 2) == column
+
+    def same_line(i):
+        return lax.rem(i // 2, 2) == line
+
+    def everything(*tests):
+        return functools.reduce(jnp.logical_and, tests)
+
+    def lacking(i):
+        return everything(spared(i), side == 1, same_column(i), same_line(i))
 
     def slab(index):
         return pl.ds(pl.multiple_of(index * rows, rows), rows)
@@ -155,47 +179,55 @@
         end = min(e for e in ends if e >= step)
         scales[1 + step] = wide(mixed(step) * (learn_rate * keep ** (end - step)))
 
-    def exchange(k, piece):
+    def exchange(k, i):
         _, distance, swap = plan[k]
         if swap:
             to = me + distance - 2 * distance * lax.rem(me // distance, 2)
         else:
             to = peer(distance)
-        cols = slice(None) if piece is None else columns(piece)
+        cols = slice(None) if i is None else columns(i)
         return pltpu.make_async_remote_copy(
             src_ref=sent.at[k, :, cols], dst_ref=arrived.at[k, :, cols],
-            send_sem=xsend.at[k], recv_sem=xrecv.at[k, 0 if piece is None else piece[2]],
+            send_sem=xsend.at[k], recv_sem=xrecv.at[k, 0 if i is None else i],
             device_id={"replica": to}, device_id_type=MESH,
         )
 
-    def gather(way, hop, piece):
+    def ring(index, cols):
+        return codes.at[slab(index), cols] if coded else out_ref.at[0, slab(index), cols]
+
+    def gather(way, hop, i, count=None):
         sign = 1 - 2 * way
-        cols, index = slice(None) if piece is None else columns(piece), z - sign * hop
-        target = out_ref.at[0, slab(index), cols]
+        cols, index = columns(i) if count is None else spread(count), z - sign * hop
+        target = ring(index, cols)
         return pltpu.make_async_remote_copy(
             src_ref=final.at[:, cols] if hop == 0 else target, dst_ref=target,
-            send_sem=zsend.at[way, hop], recv_sem=zrecv.at[way, hop, 0 if piece is None else piece[2]],
+            send_sem=zsend.at[way, hop], recv_sem=zrecv.at[way, hop, i],
             device_id={"shard": z + sign}, device_id_type=MESH,
         )
 
-    def gathered(way, hop, piece):
+    def gathered(way, hop, i):
         sign = 1 - 2 * way
-        target = out_ref.at[0, slab(z - sign * hop), columns(piece)]
+        target = ring(z - sign * hop, columns(i))
         return pltpu.make_async_remote_copy(
             src_ref=target, dst_ref=target,
-            send_sem=zsend.at[way, hop - 1], recv_sem=zrecv.at[way, hop - 1, piece[2]],
+            send_sem=zsend.at[way, hop - 1], recv_sem=zrecv.at[way, hop - 1, i],
             device_id={"shard": z - sign}, device_id_type=MESH,
         )
+
+    def outward(way):
+        return z == shards - 2 if way == 0 else z == 1
+
+    def sends(way, hop, i):
+        holds = jnp.logical_and(has_target(way), has_source(way, hop))
+        if coded:
+            holds = jnp.logical_and(holds, jnp.logical_not(jnp.logical_and(outward(way), lacking(i))))
+        return holds
 
     def has_source(way, hop):
         return z >= hop if way == 0 else z + hop < shards
 
     def has_target(way):
         return z < shards - 1 if way == 0 else z > 0
-
-    def own(piece):
-        cols = slice(None) if piece is None else columns(piece)
-        return pltpu.make_async_copy(final.at[:, cols], out_ref.at[0, slab(z), cols], own_sem)
 
     def adam(cols, known):
         m, v = first[:, cols], second[:, cols]
@@ -215,54 +247,144 @@
                 early[step - known, :, cols] = update
         return total
 
-    def tiles(piece):
-        for j in range(piece[1] // sub):
-            yield pl.ds(pl.multiple_of(piece[0] + j * sub, sub), sub)
-
-    def first_half(piece):
-        for cols in tiles(piece):
+    def tiles(i):
+        for j in range(chunk // sub):
+            yield pl.ds(pl.multiple_of(i * chunk + j * sub, sub), sub)
+
+    def first_half(i):
+        for cols in tiles(i):
             acc[:, cols] = adam(cols, 1)
 
-    def second_half(piece):
-        for cols in tiles(piece):
+    def second_half(i):
+        for cols in tiles(i):
             total = acc[:, cols]
             for step in range(1, ends[0] + 1):
                 total = total - early[step - 1, :, cols] * scales[1 + step]
             acc[:, cols] = total
             sent[0, :, cols] = encode(total)
-        exchange(0, piece).start()
-
-    def start_round(piece):
-        for cols in tiles(piece):
+        exchange(0, i).start()
+
+    def start_round(i):
+        for cols in tiles(i):
             total = adam(cols, STEPS)
             acc[:, cols] = total
             sent[0, :, cols] = encode(total)
-        exchange(0, piece).start()
-
-    def next_round(k, piece):
-        exchange(k - 1, piece).wait_recv()
-        for cols in tiles(piece):
+        exchange(0, i).start()
+
+    def next_round(k, i):
+        exchange(k - 1, i).wait_recv()
+        for cols in tiles(i):
             both = acc[:, cols] + decode(arrived[k - 1, :, cols])
             if k < rounds:
                 both = both * (0.5 * keep ** (ends[k] - ends[k - 1])) - terms[k - 1, :, cols] * scales[1 + ends[k]]
                 acc[:, cols] = both
                 sent[k, :, cols] = encode(both)
             else:
-                final[:, cols] = (both * scales[1 + STEPS]).astype(jnp.bfloat16)
+                done = (both * scales[1 + STEPS]).astype(jnp.bfloat16)
+                out_ref[0, slab(z), cols] = done
+                final[:, cols] = encode(0.5 * both) if coded else done
         if k < rounds:
-            exchange(k, piece).start()
+            exchange(k, i).start()
         else:
             for way in range(2):
-                pl.when(has_target(way))(lambda way=way: gather(way, 0, piece).start())
-            own(piece).start()
-
-    def pass_on(hop, piece):
+                pl.when(sends(way, 0, i))(lambda way=way: gather(way, 0, i).start())
+
+    def pass_on(hop, i):
         for way in range(2):
 
             @pl.when(jnp.logical_and(has_target(way), has_source(way, hop)))
             def _(way=way):
-                gathered(way, hop, piece).wait_recv()
-                gather(way, hop, piece).start()
+                gathered(way, hop, i).wait_recv()
+
+            @pl.when(sends(way, hop, i))
+            def _(way=way):
+                gather(way, hop, i).start()
+
+    def collect(i):
+        for way in range(2):
+
+            @pl.when(jnp.logical_not(has_target(way)))
+            def _(way=way):
+                for hop in range(1, shards):
+                    gathered(way, hop, i).wait_recv()
+
+    def abroad(j):
+        return slab(j + jnp.where(j >= z, 1, 0))
+
+    def relay(i, count=None):
+        cols = columns(i) if count is None else spread(count)
+        start = jnp.where(z == 0, rows, 0)
+        return pltpu.make_async_remote_copy(
+            src_ref=codes.at[pl.ds(pl.multiple_of(start, rows), foreign * rows), cols], dst_ref=extra.at[:, cols],
+            send_sem=rsend, recv_sem=rrecv.at[i],
+            device_id={"replica": me + 1 - 2 * side}, device_id_type=MESH,
+        )
+
+    def share(hop, i, count=None):
+        cols = columns(i) if count is None else spread(count)
+        to = me + 2 - 4 * column if hop else me + 4 - 8 * line
+        return pltpu.make_async_remote_copy(
+            src_ref=gap.at[:, cols], dst_ref=gaps.at[hop, :, cols],
+            send_sem=gsend.at[hop], recv_sem=grecv.at[hop, i],
+            device_id={"replica": to}, device_id_type=MESH,
+        )
+
+    def foreign_tiles(i):
+        for j in range(foreign):
+            for cols, held in zip(tiles(i), tiles(lax.rem(i, 4))):
+                yield pl.ds(j * rows, rows), abroad(j), cols, held
+
+    def put(where, cols, value):
+        out_ref[0, where, cols] = (value * scales[2 + STEPS]).astype(jnp.bfloat16)
+
+    def open_slabs(i):
+        folds = jnp.logical_and(at_end(z), spared(i))
+
+        @pl.when(jnp.logical_and(at_end(z), jnp.logical_not(lacking(i))))
+        def _():
+            collect(i)
+
+        @pl.when(jnp.logical_and(folds, side == 0))
+        def _():
+            relay(i).start()
+
+        @pl.when(jnp.logical_not(jnp.logical_and(folds, side == 1)))
+        def _():
+            for _, where, cols, _ in foreign_tiles(i):
+                put(where, cols, decode(codes[where, cols]))
+
+    def begin_fold(i):
+        @pl.when(everything(at_end(z), spared(i), side == 1, jnp.logical_not(lacking(i))))
+        def _():
+            relay(i).wait_recv()
+            for at, where, cols, held in foreign_tiles(i):
+                value = decode(codes[where, cols])
+                put(where, cols, value)
+                apart = decode(extra[at, cols]) - value
+                hold[at, held] = apart
+                gap[at, cols] = encode(apart, GAP_SCALE)
+
+            @pl.when(jnp.logical_not(same_line(i)))
+            def _():
+                share(0, i).start()
+
+    def join_fold(i):
+        @pl.when(everything(at_end(z), spared(i), side == 1, same_line(i), jnp.logical_not(same_column(i))))
+        def _():
+            share(0, i).wait_recv()
+            for at, _, cols, held in foreign_tiles(i):
+                gap[at, cols] = encode(hold[at, held] + decode(gaps[0, at, cols], GAP_SCALE), GAP_SCALE)
+            share(1, i).start()
+
+    def end_fold(i):
+        @pl.when(jnp.logical_and(at_end(z), lacking(i)))
+        def _():
+            relay(i).wait_recv()
+            share(0, i).wait_recv()
+            share(1, i).wait_recv()
+            for at, where, cols, _ in foreign_tiles(i):
+                apart = decode(gaps[0, at, cols], GAP_SCALE) + decode(gaps[1, at, cols], GAP_SCALE)
+                put(where, cols, decode(extra[at, cols]) + apart)
 
     def wait_loads(i):
         @pl.when(lax.rem(i, load_group) == 0)
@@ -276,75 +398,82 @@
         if i % load_group == 0:
             for copy in loads(i // load_group):
                 copy.wait()
-        for piece in small if i == 0 else [whole(i)]:
-            first_half(piece)
+        first_half(i)
     for step in range(1, ends[0] + 1):
         scale_of(step)
     for i in range(EARLY):
-        for piece in small if i == 0 else [whole(i)]:
-            second_half(piece)
+        second_half(i)
     wait_loads(EARLY)
-    start_round(whole(EARLY))
+    start_round(EARLY)
     for step in range(ends[0] + 1, STEPS):
         scale_of(step)
     scales[1 + STEPS] = wide(0.5 / mixed(STEPS))
+    scales[2 + STEPS] = wide(1.0 / mixed(STEPS))
 
     hops = max(shards - 2, 0)
     last = rounds * LAG
-
-    @pl.loop(EARLY + 1, chunks + last + hops * HOP_LAG)
+    late = max(last + hops * HOP_LAG, OPEN_LAG)
+
+    @pl.loop(EARLY + 1, chunks + (late + 1 + 2 * FOLD_LAG if coded else last + hops * HOP_LAG))
     def _(t):
-        def at(delay, act, low=0):
+        def at(delay, act):
             i = t - delay
-            if low == 0 and parts > 1:
-
-                @pl.when(i == 0)
-                def _():
-                    for piece in small:
-                        act(piece)
-
-                low = 1
-
-            @pl.when(jnp.logical_and(i >= low, i < chunks))
+
+            @pl.when(jnp.logical_and(i >= 0, i < chunks))
             def _():
-                act(whole(i))
+                act(i)
 
         @pl.when(t < chunks)
         def _():
             wait_loads(t)
-            start_round(whole(t))
+            start_round(t)
 
         for k in range(1, rounds + 1):
             at(k * LAG, functools.partial(next_round, k))
         for hop in range(1, hops + 1):
             at(last + hop * HOP_LAG, functools.partial(pass_on, hop))
-
-    for way in range(2):
-
-        @pl.when(jnp.logical_not(has_target(way)))
-        def _(way=way):
-            def drain(piece):
-                for hop in range(1, shards):
-                    pl.when(has_source(way, hop))(lambda hop=hop: gathered(way, hop, piece).wait_recv())
-
-            for piece in small:
-                drain(piece)
-
-            @pl.loop(1, chunks)
-            def _(i):
-                drain(whole(i))
+        if coded:
+            at(late, open_slabs)
+            at(late + 1, begin_fold)
+            at(late + 1 + FOLD_LAG, join_fold)
+            at(late + 1 + 2 * FOLD_LAG, end_fold)
+
+    if not coded:
+
+        @pl.loop(0, chunks)
+        def _(i):
+            collect(i)
 
     for k in range(1, replicas):
         weight_copy(k, me).wait_send()
     for k in range(rounds):
         exchange(k, None).wait_send()
-    own(None).wait()
     for way in range(2):
         for hop in range(shards - 1):
-
-            @pl.when(jnp.logical_and(has_target(way), has_source(way, hop)))
+            holds = jnp.logical_and(has_target(way), has_source(way, hop))
+            if coded:
+                less = jnp.logical_and(outward(way), side == 1)
+
+                @pl.when(jnp.logical_and(holds, less))
+                def _(way=way, hop=hop):
+                    gather(way, hop, 0, chunks - spares).wait_send()
+
+                holds = jnp.logical_and(holds, jnp.logical_not(less))
+
+            @pl.when(holds)
             def _(way=way, hop=hop):
-                gather(way, hop, None).wait_send()
+                gather(way, hop, 0, chunks).wait_send()
+
+    if coded:
+
+        @pl.when(jnp.logical_and(at_end(z), side == 0))
+        def _():
+            relay(0, 4 * spares).wait_send()
+
+        @pl.when(jnp.logical_and(at_end(z), side == 1))
+        def _():
+            share(0, 0, 2 * spares).wait_send()
+            share(1, 0, spares).wait_send()
 
 
 def per_device(params, first_moment, second_moment, grads, push_weight):
@@ -353,30 +482,42 @@
     units = cols // 128
     chunks = max(n for n in range(1, CHUNKS + 1) if units % n == 0)
     chunk = cols // chunks
-    parts = PARTS if chunk % (128 * PARTS) == 0 else 1
-    sub = max(128 * n for n in range(1, SUB + 1) if (chunk // parts) % (128 * n) == 0)
+    sub = max(128 * n for n in range(1, SUB + 1) if chunk % (128 * n) == 0)
     load_group = LOAD_GROUP if chunks % LOAD_GROUP == 0 else 1
     plan, mixes = plan_of(replicas), mixes_of(replicas)
     rounds = len(plan)
-    pieces = chunks + parts - 1
+    alternate = replicas == 8 and plan[-1][1] == 1 and not plan[-1][2] and shards > 2
+    spares = max(chunks - 1 - FULL_TAIL, 0) // 4 if alternate else 0
     f32, bf16, dma = jnp.float32, jnp.bfloat16, pltpu.SemaphoreType.DMA
     anywhere = pl.BlockSpec(memory_space=pl.ANY)
-    body = functools.partial(kernel, plan, mixes, replicas, shards, chunks, chunk, parts, sub, load_group)
+    body = functools.partial(kernel, plan, mixes, replicas, shards, chunks, chunk, sub, load_group, spares)
     hops = max(shards - 1, 1)
     large = (params, first_moment, second_moment, grads)
     large = tuple(pltpu.with_memory_space_constraint(x, pltpu.HBM) for x in large)
+    apart = (shards - 1) * rows
+    folding = (
+        pltpu.VMEM((shards * rows, cols), bf16),
+        pltpu.VMEM((apart, cols), bf16),
+        pltpu.VMEM((apart, 4 * chunk), f32),
+        pltpu.VMEM((apart, cols), bf16),
+        pltpu.VMEM((2, apart, cols), bf16),
+        dma,
+        dma((chunks,)),
+        dma((2,)),
+        dma((2, chunks)),
+    )
     return pl.pallas_call(
         body,
         out_shape=jax.ShapeDtypeStruct((1, rows * shards, cols), bf16),
         in_specs=[anywhere] * 4 + [pl.BlockSpec(memory_space=pltpu.SMEM)],
-        out_specs=anywhere,
+        out_specs=pl.BlockSpec(memory_space=pltpu.VMEM),
         scratch_shapes=[
             pltpu.VMEM((rows, cols), f32),
             pltpu.VMEM((rows, cols), f32),
             pltpu.VMEM((rows, cols), f32),
             pltpu.VMEM((STEPS, rows, cols), bf16),
             pltpu.VMEM((replicas, 8, 128), f32),
-            pltpu.VMEM((STEPS + 2, rows, sub), f32),
+            pltpu.VMEM((STEPS + 3, rows, sub), f32),
             pltpu.VMEM((rows, cols), f32),
             pltpu.VMEM((max(rounds - 1, 1), rows, cols), f32),
             pltpu.VMEM((max(plan[0][0], 1), rows, EARLY * chunk), f32),
@@ -387,10 +528,10 @@
             dma((replicas - 1,)),
             dma((replicas - 1,)),
             dma((rounds,)),
-            dma((rounds, pieces)),
+            dma((rounds, chunks)),
             dma((2, hops)),
-            dma((2, hops, pieces)),
-            dma,
+            dma((2, hops, chunks)),
+            *(folding if spares else ()),
         ],
         compiler_params=pltpu.CompilerParams(
             collective_id=0, has_side_effects=True, vmem_limit_bytes=48 * 1024 * 1024

time: 81.8 us -> 84 us (1.027)
  the two profiles are of different devices: /device:TPU:0 before, /device:TPU:1 now
where the time goes in v2:
time: 84 us; the launch traced here: 83.9 us
  Pallas kernels  81.4 us (97%)
  local copies, waits for them, and re-layouts  1.84 us (2%)
    pallas_call x1, Pallas kernels, per_device(): pl.pallas_call(body, out_shape=jax.ShapeDtypeStruct((1, rows * shards, co...  81.4 us
    unnamed x1, local copies, waits for them, and re-layouts  1.84 us

profile of v2, /device:TPU:1, one launch (start us, length us, event | category | flops | bytes accessed | tf_op | source)
XLA Modules:
  0.0 83.9 jit_solution(10724912225296078746)
XLA Ops:
  0.7 81.4 %shard_map.55 = bf16[1,64,28672]{2,1,0:T(8,128)(2,1)S(1)} custom-call(f32[1,16,28672]{2,1,0:T(8,128)} %params_ref.1, f32[1,16,28672]{2,1,0:T(8,128)} %first_ref.1, f32[1,16,28672]{2,1,0:T(8,128)} %second_ref.1, bf16[4,1,16,28672]{3,2,1,0:T(8,128)(2,1)} %grads_ref.1, f32[1]{0:T(128)S(6)} %copy.7.weight_ref), custom_call_target="tpu_custom_call" | custom-call | tf_op jit(solution)/shard_map/pallas_call | solution.py:509
  82.0 1.8 %copy.8 = bf16[1,64,28672]{2,1,0:T(8,128)(2,1)} copy(bf16[1,64,28672]{2,1,0:T(8,128)(2,1)S(1)} %shard_map.55) | data formatting | bytes 7340032

commit v3 on v2

--- a/solution.py
+++ b/solution.py
@@ -23,8 +23,9 @@
 HOP_LAG = 2
 CHUNKS = 28
 OPEN_LAG = 18
-FOLD_LAG = 2
+FOLD_LAG = 3
 FULL_TAIL = 3
+EAGER = 14
 EARLY = 2
 LOAD_GROUP = 2
 SUB = 2
@@ -102,16 +103,19 @@
         return jnp.logical_and(i >= 1, i <= 4 * spares)
 
     def same_column(i):
-        return lax.rem(i, 2) == column
+        return lax.rem(i - 1, 2) == column
 
     def same_line(i):
-        return lax.rem(i // 2, 2) == line
+        return lax.rem((i - 1) // 2, 2) == line
+
+    def folded_here(i):
+        return lax.rem((i - 1) // 4, 2) == side
 
     def everything(*tests):
         return functools.reduce(jnp.logical_and, tests)
 
     def lacking(i):
-        return everything(spared(i), side == 1, same_column(i), same_line(i))
+        return everything(spared(i), folded_here(i), same_column(i), same_line(i))
 
     def slab(index):
         return pl.ds(pl.multiple_of(index * rows, rows), rows)
@@ -216,6 +220,9 @@
 
     def outward(way):
         return z == shards - 2 if way == 0 else z == 1
+
+    def eager(way, i):
+        return jnp.logical_or(i < EAGER, jnp.logical_not(outward(way))) if coded else i >= 0
 
     def sends(way, hop, i):
         holds = jnp.logical_and(has_target(way), has_source(way, hop))
@@ -287,18 +294,31 @@
             exchange(k, i).start()
         else:
             for way in range(2):
-                pl.when(sends(way, 0, i))(lambda way=way: gather(way, 0, i).start())
+                pl.when(everything(sends(way, 0, i), eager(way, i)))(lambda way=way: gather(way, 0, i).start())
 
     def pass_on(hop, i):
         for way in range(2):
 
-            @pl.when(jnp.logical_and(has_target(way), has_source(way, hop)))
+            @pl.when(everything(has_target(way), has_source(way, hop), eager(way, i)))
             def _(way=way):
                 gathered(way, hop, i).wait_recv()
 
-            @pl.when(sends(way, hop, i))
+            @pl.when(everything(sends(way, hop, i), eager(way, i)))
             def _(way=way):
                 gather(way, hop, i).start()
+
+    def send_out(i):
+        for way in range(2):
+
+            @pl.when(everything(has_target(way), outward(way), i >= EAGER))
+            def _(way=way):
+                pl.when(sends(way, 0, i))(lambda: gather(way, 0, i).start())
+                for hop in range(1, shards - 1):
+
+                    @pl.when(has_source(way, hop))
+                    def _(hop=hop):
+                        gathered(way, hop, i).wait_recv()
+                        pl.when(sends(way, hop, i))(lambda: gather(way, hop, i).start())
 
     def collect(i):
         for way in range(2):
@@ -331,7 +351,7 @@
 
     def foreign_tiles(i):
         for j in range(foreign):
-            for cols, held in zip(tiles(i), tiles(lax.rem(i, 4))):
+            for cols, held in zip(tiles(i), tiles(lax.rem(i, 8))):
                 yield pl.ds(j * rows, rows), abroad(j), cols, held
 
     def put(where, cols, value):
@@ -344,17 +364,17 @@
         def _():
             collect(i)
 
-        @pl.when(jnp.logical_and(folds, side == 0))
+        @pl.when(jnp.logical_and(folds, jnp.logical_not(folded_here(i))))
         def _():
             relay(i).start()
 
-        @pl.when(jnp.logical_not(jnp.logical_and(folds, side == 1)))
+        @pl.when(jnp.logical_not(jnp.logical_and(folds, folded_here(i))))
         def _():
             for _, where, cols, _ in foreign_tiles(i):
                 put(where, cols, decode(codes[where, cols]))
 
     def begin_fold(i):
-        @pl.when(everything(at_end(z), spared(i), side == 1, jnp.logical_not(lacking(i))))
+        @pl.when(everything(at_end(z), spared(i), folded_here(i), jnp.logical_not(lacking(i))))
         def _():
             relay(i).wait_recv()
             for at, where, cols, held in foreign_tiles(i):
@@ -369,7 +389,7 @@
                 share(0, i).start()
 
     def join_fold(i):
-        @pl.when(everything(at_end(z), spared(i), side == 1, same_line(i), jnp.logical_not(same_column(i))))
+        @pl.when(everything(at_end(z), spared(i), folded_here(i), same_line(i), jnp.logical_not(same_column(i))))
         def _():
             share(0, i).wait_recv()
             for at, _, cols, held in foreign_tiles(i):
@@ -410,11 +430,20 @@
     scales[1 + STEPS] = wide(0.5 / mixed(STEPS))
     scales[2 + STEPS] = wide(1.0 / mixed(STEPS))
 
+    def catch_up(slot, final_slot, delay, act):
+        until = jnp.where(slot == final_slot, 4 * spares + 1, slot - delay)
+
+        @pl.when(jnp.logical_and(slot > delay, slot <= final_slot))
+        def _():
+            @pl.loop(slot - 1 - delay, until)
+            def _(i):
+                act(i)
+
     hops = max(shards - 2, 0)
     last = rounds * LAG
     late = max(last + hops * HOP_LAG, OPEN_LAG)
 
-    @pl.loop(EARLY + 1, chunks + (late + 1 + 2 * FOLD_LAG if coded else last + hops * HOP_LAG))
+    @pl.loop(EARLY + 1, chunks + (late + 1 if coded else last + hops * HOP_LAG))
     def _(t):
         def at(delay, act):
             i = t - delay
@@ -433,10 +462,11 @@
         for hop in range(1, hops + 1):
             at(last + hop * HOP_LAG, functools.partial(pass_on, hop))
         if coded:
+            at(last + hops * HOP_LAG, send_out)
+            at(late + 1, begin_fold)
+            catch_up(t - late, chunks - 1, FOLD_LAG, join_fold)
+            catch_up(t - late, chunks, 2 * FOLD_LAG, end_fold)
             at(late, open_slabs)
-            at(late + 1, begin_fold)
-            at(late + 1 + FOLD_LAG, join_fold)
-            at(late + 1 + 2 * FOLD_LAG, end_fold)
 
     if not coded:
 
@@ -452,11 +482,11 @@
         for hop in range(shards - 1):
             holds = jnp.logical_and(has_target(way), has_source(way, hop))
             if coded:
-                less = jnp.logical_and(outward(way), side == 1)
+                less = outward(way)
 
                 @pl.when(jnp.logical_and(holds, less))
                 def _(way=way, hop=hop):
-                    gather(way, hop, 0, chunks - spares).wait_send()
+                    gather(way, hop, 0, chunks - spares // 2).wait_send()
 
                 holds = jnp.logical_and(holds, jnp.logical_not(less))
 
@@ -466,14 +496,11 @@
 
     if coded:
 
-        @pl.when(jnp.logical_and(at_end(z), side == 0))
-        def _():
-            relay(0, 4 * spares).wait_send()
-
-        @pl.when(jnp.logical_and(at_end(z), side == 1))
-        def _():
-            share(0, 0, 2 * spares).wait_send()
-            share(1, 0, spares).wait_send()
+        @pl.when(at_end(z))
+        def _():
+            relay(0, 2 * spares).wait_send()
+            share(0, 0, spares).wait_send()
+            share(1, 0, spares // 2).wait_send()
 
 
 def per_device(params, first_moment, second_moment, grads, push_weight):
@@ -487,7 +514,7 @@
     plan, mixes = plan_of(replicas), mixes_of(replicas)
     rounds = len(plan)
     alternate = replicas == 8 and plan[-1][1] == 1 and not plan[-1][2] and shards > 2
-    spares = max(chunks - 1 - FULL_TAIL, 0) // 4 if alternate else 0
+    spares = max(chunks - 1 - FULL_TAIL, 0) // 8 * 2 if alternate else 0
     f32, bf16, dma = jnp.float32, jnp.bfloat16, pltpu.SemaphoreType.DMA
     anywhere = pl.BlockSpec(memory_space=pl.ANY)
     body = functools.partial(kernel, plan, mixes, replicas, shards, chunks, chunk, sub, load_group, spares)
@@ -498,7 +525,7 @@
     folding = (
         pltpu.VMEM((shards * rows, cols), bf16),
         pltpu.VMEM((apart, cols), bf16),
-        pltpu.VMEM((apart, 4 * chunk), f32),
+        pltpu.VMEM((apart, 8 * chunk), f32),
         pltpu.VMEM((apart, cols), bf16),
         pltpu.VMEM((2, apart, cols), bf16),
         dma,

time: 84 us -> 77.6 us (0.924)
  the two profiles are of different devices: /device:TPU:1 before, /device:TPU:0 now
where the time goes in v3:
time: 77.6 us; the launch traced here: 76.8 us
  Pallas kernels  74.3 us (96%)
  local copies, waits for them, and re-layouts  1.84 us (2%)
    pallas_call x1, Pallas kernels, per_device(): pl.pallas_call(body, out_shape=jax.ShapeDtypeStruct((1, rows * shards, co...  74.3 us
    unnamed x1, local copies, waits for them, and re-layouts  1.84 us

profile of v3, /device:TPU:0, one launch (start us, length us, event | category | flops | bytes accessed | tf_op | source)
XLA Modules:
  0.0 76.8 jit_solution(14535327617197499872)
XLA Ops:
  0.7 74.3 %shard_map.55 = bf16[1,64,28672]{2,1,0:T(8,128)(2,1)S(1)} custom-call(f32[1,16,28672]{2,1,0:T(8,128)} %params_ref.1, f32[1,16,28672]{2,1,0:T(8,128)} %first_ref.1, f32[1,16,28672]{2,1,0:T(8,128)} %second_ref.1, bf16[4,1,16,28672]{3,2,1,0:T(8,128)(2,1)} %grads_ref.1, f32[1]{0:T(128)S(6)} %copy.7.weight_ref), custom_call_target="tpu_custom_call" | custom-call | tf_op jit(solution)/shard_map/pallas_call | solution.py:536
  75.0 1.8 %copy.8 = bf16[1,64,28672]{2,1,0:T(8,128)(2,1)} copy(bf16[1,64,28672]{2,1,0:T(8,128)(2,1)S(1)} %shard_map.55) | data formatting | bytes 7340032

commit v4 on v3

--- a/solution.py
+++ b/solution.py
@@ -20,10 +20,14 @@
 CODE_SCALE = 8.0
 GAP_SCALE = 16.0
 LAG = 3
-HOP_LAG = 2
+HOP_LAG = 3
+NEXT_HOP_LAG = 3
 CHUNKS = 28
-OPEN_LAG = 18
+OPEN_LAG = 20
 FOLD_LAG = 3
+SWIFT = 1
+SWIFT_AT = 17
+SWIFT_LAG = 3
 FULL_TAIL = 3
 EAGER = 14
 EARLY = 2
@@ -58,6 +62,10 @@
     return mixes
 
 
+def hop_lag(hop):
+    return HOP_LAG + (hop - 1) * NEXT_HOP_LAG if hop else 0
+
+
 def encode(value, scale=CODE_SCALE):
     power = value * scale
     power = power * power
@@ -79,7 +87,8 @@
     params, first, second, grads, weights, scales, acc, terms, early, sent, arrived, final,
     load_sem, wsend, wrecv, xsend, xrecv, zsend, zrecv,
     codes=None, extra=None, hold=None, gap=None, gaps=None,
-    rsend=None, rrecv=None, gsend=None, grecv=None,
+    beside=None,
+    rsend=None, rrecv=None, gsend=None, grecv=None, bsend=None, brecv=None,
 ):
     me, z = lax.axis_index("replica"), lax.axis_index("shard")
     rows = params.shape[0]
@@ -87,6 +96,7 @@
     ends = [step for step, _, _ in plan]
     keep = 1.0 - learn_rate * decay_rate
     coded = spares > 0
+    swift = SWIFT if coded else 0
     side, column, line = lax.rem(me, 2), lax.rem(me // 2, 2), me // 4
     foreign = shards - 1
 
@@ -100,16 +110,16 @@
         return jnp.logical_or(z == 0, z == shards - 1)
 
     def spared(i):
-        return jnp.logical_and(i >= 1, i <= 4 * spares)
+        return jnp.logical_and(i >= swift, i < swift + 4 * spares)
 
     def same_column(i):
-        return lax.rem(i - 1, 2) == column
+        return lax.rem(i - swift, 2) == column
 
     def same_line(i):
-        return lax.rem((i - 1) // 2, 2) == line
+        return lax.rem((i - swift) // 2, 2) == line
 
     def folded_here(i):
-        return lax.rem((i - 1) // 4, 2) == side
+        return lax.rem((i - swift) // 4, 2) == side
 
     def everything(*tests):
         return functools.reduce(jnp.logical_and, tests)
@@ -199,12 +209,12 @@
     def ring(index, cols):
         return codes.at[slab(index), cols] if coded else out_ref.at[0, slab(index), cols]
 
-    def gather(way, hop, i, count=None):
+    def gather(way, hop, i, count=None, early=False):
         sign = 1 - 2 * way
         cols, index = columns(i) if count is None else spread(count), z - sign * hop
         target = ring(index, cols)
         return pltpu.make_async_remote_copy(
-            src_ref=final.at[:, cols] if hop == 0 else target, dst_ref=target,
+            src_ref=target if hop else sent.at[rounds - 1, :, cols] if early else final.at[:, cols], dst_ref=target,
             send_sem=zsend.at[way, hop], recv_sem=zrecv.at[way, hop, i],
             device_id={"shard": z + sign}, device_id_type=MESH,
         )
@@ -292,9 +302,12 @@
                 final[:, cols] = encode(0.5 * both) if coded else done
         if k < rounds:
             exchange(k, i).start()
+            if k == rounds - 1 and swift:
+                for way in range(2):
+                    pl.when(jnp.logical_and(has_target(way), i < swift))(lambda way=way: gather(way, 0, i, early=True).start())
         else:
             for way in range(2):
-                pl.when(everything(sends(way, 0, i), eager(way, i)))(lambda way=way: gather(way, 0, i).start())
+                pl.when(everything(sends(way, 0, i), eager(way, i), i >= swift))(lambda way=way: gather(way, 0, i).start())
 
     def pass_on(hop, i):
         for way in range(2):
@@ -348,6 +361,28 @@
             send_sem=gsend.at[hop], recv_sem=grecv.at[hop, i],
             device_id={"replica": to}, device_id_type=MESH,
         )
+
+    def lend(i, j):
+        return pltpu.make_async_remote_copy(
+            src_ref=codes.at[abroad(j), columns(i)], dst_ref=beside.at[pl.ds(j * rows, rows), columns(i)],
+            send_sem=bsend, recv_sem=brecv.at[i * foreign + j],
+            device_id={"replica": peer(1)}, device_id_type=MESH,
+        )
+
+    def lend_swift(i):
+        @pl.when(at_end(z))
+        def _():
+            collect(i)
+
+        for j in range(foreign):
+            lend(i, j).start()
+
+    def open_swift(i):
+        for j in range(foreign):
+            lend(i, j).wait_recv()
+        for at, where, cols, _ in foreign_tiles(i):
+            both = decode(codes[where, cols]) + decode(beside[at, cols])
+            out_ref[0, where, cols] = (both * scales[1 + STEPS]).astype(jnp.bfloat16)
 
     def foreign_tiles(i):
         for j in range(foreign):
@@ -431,7 +466,7 @@
     scales[2 + STEPS] = wide(1.0 / mixed(STEPS))
 
     def catch_up(slot, final_slot, delay, act):
-        until = jnp.where(slot == final_slot, 4 * spares + 1, slot - delay)
+        until = jnp.where(slot == final_slot, 4 * spares + swift, slot - delay)
 
         @pl.when(jnp.logical_and(slot > delay, slot <= final_slot))
         def _():
@@ -441,14 +476,14 @@
 
     hops = max(shards - 2, 0)
     last = rounds * LAG
-    late = max(last + hops * HOP_LAG, OPEN_LAG)
-
-    @pl.loop(EARLY + 1, chunks + (late + 1 if coded else last + hops * HOP_LAG))
+    late = max(last + hop_lag(hops), OPEN_LAG)
+
+    @pl.loop(EARLY + 1, chunks + (late + 1 if coded else last + hop_lag(hops)))
     def _(t):
-        def at(delay, act):
+        def at(delay, act, low=0, high=chunks):
             i = t - delay
 
-            @pl.when(jnp.logical_and(i >= 0, i < chunks))
+            @pl.when(jnp.logical_and(i >= low, i < high))
             def _():
                 act(i)
 
@@ -460,13 +495,17 @@
         for k in range(1, rounds + 1):
             at(k * LAG, functools.partial(next_round, k))
         for hop in range(1, hops + 1):
-            at(last + hop * HOP_LAG, functools.partial(pass_on, hop))
+            at(last + hop_lag(hop), functools.partial(pass_on, hop), swift)
+            if swift:
+                at(last - LAG + hop_lag(hop), functools.partial(pass_on, hop), 0, swift)
         if coded:
-            at(last + hops * HOP_LAG, send_out)
+            at(last + hop_lag(hops), send_out)
             at(late + 1, begin_fold)
             catch_up(t - late, chunks - 1, FOLD_LAG, join_fold)
             catch_up(t - late, chunks, 2 * FOLD_LAG, end_fold)
-            at(late, open_slabs)
+            at(late, open_slabs, swift)
+            at(SWIFT_AT, lend_swift, 0, swift)
+            at(SWIFT_AT + SWIFT_LAG, open_swift, 0, swift)
 
     if not coded:
 
@@ -501,6 +540,11 @@
             relay(0, 2 * spares).wait_send()
             share(0, 0, spares).wait_send()
             share(1, 0, spares // 2).wait_send()
+
+        pltpu.make_async_remote_copy(
+            src_ref=beside, dst_ref=beside, send_sem=bsend, recv_sem=brecv.at[0],
+            device_id={"replica": peer(1)}, device_id_type=MESH,
+        ).wait_send()
 
 
 def per_device(params, first_moment, second_moment, grads, push_weight):
@@ -514,7 +558,7 @@
     plan, mixes = plan_of(replicas), mixes_of(replicas)
     rounds = len(plan)
     alternate = replicas == 8 and plan[-1][1] == 1 and not plan[-1][2] and shards > 2
-    spares = max(chunks - 1 - FULL_TAIL, 0) // 8 * 2 if alternate else 0
+    spares = max(chunks - SWIFT - FULL_TAIL, 0) // 8 * 2 if alternate else 0
     f32, bf16, dma = jnp.float32, jnp.bfloat16, pltpu.SemaphoreType.DMA
     anywhere = pl.BlockSpec(memory_space=pl.ANY)
     body = functools.partial(kernel, plan, mixes, replicas, shards, chunks, chunk, sub, load_group, spares)
@@ -528,10 +572,13 @@
         pltpu.VMEM((apart, 8 * chunk), f32),
         pltpu.VMEM((apart, cols), bf16),
         pltpu.VMEM((2, apart, cols), bf16),
+        pltpu.VMEM((apart, SWIFT * chunk), bf16),
         dma,
         dma((chunks,)),
         dma((2,)),
         dma((2, chunks)),
+        dma,
+        dma((SWIFT * (shards - 1),)),
     )
     return pl.pallas_call(
         body,

time: 77.6 us -> 77.1 us (level)
  no operation moved by 1% of the time
where the time goes in v4:
time: 77.1 us; the launch traced here: 76.6 us
  Pallas kernels  74.1 us (96%)
  local copies, waits for them, and re-layouts  1.84 us (2%)
    pallas_call x1, Pallas kernels, per_device(): pl.pallas_call(body, out_shape=jax.ShapeDtypeStruct((1, rows * shards, co...  74.1 us
    unnamed x1, local copies, waits for them, and re-layouts  1.84 us

profile of v4, /device:TPU:0, one launch (start us, length us, event | category | flops | bytes accessed | tf_op | source)
XLA Modules:
  0.0 76.6 jit_solution(2783784423918239814)
XLA Ops:
  0.7 74.1 %shard_map.55 = bf16[1,64,28672]{2,1,0:T(8,128)(2,1)S(1)} custom-call(f32[1,16,28672]{2,1,0:T(8,128)} %params_ref.1, f32[1,16,28672]{2,1,0:T(8,128)} %first_ref.1, f32[1,16,28672]{2,1,0:T(8,128)} %second_ref.1, bf16[4,1,16,28672]{3,2,1,0:T(8,128)(2,1)} %grads_ref.1, f32[1]{0:T(128)S(6)} %copy.7.weight_ref), custom_call_target="tpu_custom_call" | custom-call | tf_op jit(solution)/shard_map/pallas_call | solution.py:583
  74.8 1.8 %copy.8 = bf16[1,64,28672]{2,1,0:T(8,128)(2,1)} copy(bf16[1,64,28672]{2,1,0:T(8,128)(2,1)S(1)} %shard_map.55) | data formatting | bytes 7340032

commit v5 on v4

--- a/solution.py
+++ b/solution.py
@@ -31,7 +31,7 @@
 FULL_TAIL = 3
 EAGER = 14
 EARLY = 2
-LOAD_GROUP = 2
+LOAD_GROUP = 4
 SUB = 2
 MESH = pl.DeviceIdType.MESH
 
@@ -89,6 +89,7 @@
     codes=None, extra=None, hold=None, gap=None, gaps=None,
     beside=None,
     rsend=None, rrecv=None, gsend=None, grecv=None, bsend=None, brecv=None,
+    lead=None, lsend=None, lrecv=None,
 ):
     me, z = lax.axis_index("replica"), lax.axis_index("shard")
     rows = params.shape[0]
@@ -97,6 +98,7 @@
     keep = 1.0 - learn_rate * decay_rate
     coded = spares > 0
     swift = SWIFT if coded else 0
+    leads = coded and ends[0] == 1 and plan[0][2]
     side, column, line = lax.rem(me, 2), lax.rem(me // 2, 2), me // 4
     foreign = shards - 1
 
@@ -193,12 +195,30 @@
         end = min(e for e in ends if e >= step)
         scales[1 + step] = wide(mixed(step) * (learn_rate * keep ** (end - step)))
 
+    def partner(k):
+        _, distance, swap = plan[k]
+        return me + distance - 2 * distance * lax.rem(me // distance, 2) if swap else peer(distance)
+
+    def lead_copy():
+        return pltpu.make_async_remote_copy(
+            src_ref=lead.at[0], dst_ref=lead.at[1], send_sem=lsend, recv_sem=lrecv,
+            device_id={"replica": partner(0)}, device_id_type=MESH,
+        )
+
+    def start_early():
+        for cols in tiles(0):
+            sent[0, :, cols] = encode(acc[:, cols])
+            lead[0, :, cols] = encode(early[0, :, cols])
+        exchange(0, 0).start()
+        lead_copy().start()
+
+    def finish_early():
+        lead_copy().wait_recv()
+        for cols in tiles(0):
+            acc[:, cols] = acc[:, cols] - decode(lead[1, :, cols]) * scales[3 + STEPS]
+
     def exchange(k, i):
-        _, distance, swap = plan[k]
-        if swap:
-            to = me + distance - 2 * distance * lax.rem(me // distance, 2)
-        else:
-            to = peer(distance)
+        to = partner(k)
         cols = slice(None) if i is None else columns(i)
         return pltpu.make_async_remote_copy(
             src_ref=sent.at[k, :, cols], dst_ref=arrived.at[k, :, cols],
@@ -278,8 +298,10 @@
             for step in range(1, ends[0] + 1):
                 total = total - early[step - 1, :, cols] * scales[1 + step]
             acc[:, cols] = total
-            sent[0, :, cols] = encode(total)
-        exchange(0, i).start()
+            if not (leads and i == 0):
+                sent[0, :, cols] = encode(total)
+        if not (leads and i == 0):
+            exchange(0, i).start()
 
     def start_round(i):
         for cols in tiles(i):
@@ -290,6 +312,8 @@
 
     def next_round(k, i):
         exchange(k - 1, i).wait_recv()
+        if k == 1 and leads:
+            pl.when(i == 0)(finish_early)
         for cols in tiles(i):
             both = acc[:, cols] + decode(arrived[k - 1, :, cols])
             if k < rounds:
@@ -454,6 +478,8 @@
             for copy in loads(i // load_group):
                 copy.wait()
         first_half(i)
+        if leads and i == 0:
+            start_early()
     for step in range(1, ends[0] + 1):
         scale_of(step)
     for i in range(EARLY):
@@ -464,6 +490,9 @@
         scale_of(step)
     scales[1 + STEPS] = wide(0.5 / mixed(STEPS))
     scales[2 + STEPS] = wide(1.0 / mixed(STEPS))
+    if leads:
+        theirs = sum(share * weights[lax.rem(partner(0) - k + replicas, replicas)] for k, share in mixes[1].items())
+        scales[3 + STEPS] = wide(theirs * learn_rate)
 
     def catch_up(slot, final_slot, delay, act):
         until = jnp.where(slot == final_slot, 4 * spares + swift, slot - delay)
@@ -541,6 +570,8 @@
             share(0, 0, spares).wait_send()
             share(1, 0, spares // 2).wait_send()
 
+        if leads:
+            lead_copy().wait_send()
         pltpu.make_async_remote_copy(
             src_ref=beside, dst_ref=beside, send_sem=bsend, recv_sem=brecv.at[0],
             device_id={"replica": peer(1)}, device_id_type=MESH,
@@ -579,6 +610,9 @@
         dma((2, chunks)),
         dma,
         dma((SWIFT * (shards - 1),)),
+        pltpu.VMEM((2, rows, chunk), bf16),
+        dma,
+        dma,
     )
     return pl.pallas_call(
         body,
@@ -591,7 +625,7 @@
             pltpu.VMEM((rows, cols), f32),
             pltpu.VMEM((STEPS, rows, cols), bf16),
             pltpu.VMEM((replicas, 8, 128), f32),
-            pltpu.VMEM((STEPS + 3, rows, sub), f32),
+            pltpu.VMEM((STEPS + 4, rows, sub), f32),
             pltpu.VMEM((rows, cols), f32),
             pltpu.VMEM((max(rounds - 1, 1), rows, cols), f32),
             pltpu.VMEM((max(plan[0][0], 1), rows, EARLY * chunk), f32),

time: 77.1 us -> 76.2 us (0.988)
  Pallas kernels: 74.1 us -> 73 us
    pallas_call x1, Pallas kernels: 74.1 us -> 73 us  [per_device(): pl.pallas_call(body, out_shape=jax.ShapeDtypeStruct((1, rows * shards, co...]
where the time goes in v5:
time: 76.2 us; the launch traced here: 75.5 us
  Pallas kernels  73 us (96%)
  local copies, waits for them, and re-layouts  1.84 us (2%)
    pallas_call x1, Pallas kernels, per_device(): pl.pallas_call(body, out_shape=jax.ShapeDtypeStruct((1, rows * shards, co...  73 us
    unnamed x1, local copies, waits for them, and re-layouts  1.84 us

profile of v5, /device:TPU:0, one launch (start us, length us, event | category | flops | bytes accessed | tf_op | source)
XLA Modules:
  0.0 75.5 jit_solution(2281425686369559002)
XLA Ops:
  0.7 73.0 %shard_map.55 = bf16[1,64,28672]{2,1,0:T(8,128)(2,1)S(1)} custom-call(f32[1,16,28672]{2,1,0:T(8,128)} %params_ref.1, f32[1,16,28672]{2,1,0:T(8,128)} %first_ref.1, f32[1,16,28672]{2,1,0:T(8,128)} %second_ref.1, bf16[4,1,16,28672]{3,2,1,0:T(8,128)(2,1)} %grads_ref.1, f32[1]{0:T(128)S(6)} %copy.7.weight_ref), custom_call_target="tpu_custom_call" | custom-call | tf_op jit(solution)/shard_map/pallas_call | solution.py:617
  73.7 1.8 %copy.8 = bf16[1,64,28672]{2,1,0:T(8,128)(2,1)} copy(bf16[1,64,28672]{2,1,0:T(8,128)(2,1)S(1)} %shard_map.55) | data formatting | bytes 7340032

commit v6 on v5

--- a/solution.py
+++ b/solution.py
@@ -29,10 +29,10 @@
 SWIFT_AT = 17
 SWIFT_LAG = 3
 FULL_TAIL = 3
-EAGER = 14
+EAGER = 17
 EARLY = 2
 LOAD_GROUP = 4
-SUB = 2
+SUB = 4
 MESH = pl.DeviceIdType.MESH
 
 

time: 76.2 us -> 76.4 us (level)
  no operation moved by 1% of the time
where the time goes in v6:
time: 76.4 us; the launch traced here: 75.5 us
  Pallas kernels  73 us (96%)
  local copies, waits for them, and re-layouts  1.84 us (2%)
    pallas_call x1, Pallas kernels, per_device(): pl.pallas_call(body, out_shape=jax.ShapeDtypeStruct((1, rows * shards, co...  73 us
    unnamed x1, local copies, waits for them, and re-layouts  1.84 us

profile of v6, /device:TPU:0, one launch (start us, length us, event | category | flops | bytes accessed | tf_op | source)
XLA Modules:
  0.0 75.5 jit_solution(791731425239804130)
XLA Ops:
  0.7 73.0 %shard_map.55 = bf16[1,64,28672]{2,1,0:T(8,128)(2,1)S(1)} custom-call(f32[1,16,28672]{2,1,0:T(8,128)} %params_ref.1, f32[1,16,28672]{2,1,0:T(8,128)} %first_ref.1, f32[1,16,28672]{2,1,0:T(8,128)} %second_ref.1, bf16[4,1,16,28672]{3,2,1,0:T(8,128)(2,1)} %grads_ref.1, f32[1]{0:T(128)S(6)} %copy.7.weight_ref), custom_call_target="tpu_custom_call" | custom-call | tf_op jit(solution)/shard_map/pallas_call | solution.py:617
  73.7 1.8 %copy.8 = bf16[1,64,28672]{2,1,0:T(8,128)(2,1)} copy(bf16[1,64,28672]{2,1,0:T(8,128)(2,1)S(1)} %shard_map.55) | data formatting | bytes 7340032

commit v7 on v5

--- a/solution.py
+++ b/solution.py
@@ -24,7 +24,7 @@
 NEXT_HOP_LAG = 3
 CHUNKS = 28
 OPEN_LAG = 20
-FOLD_LAG = 3
+FOLD_LAG = 4
 SWIFT = 1
 SWIFT_AT = 17
 SWIFT_LAG = 3

time: 76.2 us -> 76.2 us (level)
  no operation moved by 1% of the time
where the time goes in v7:
time: 76.2 us; the launch traced here: 75.6 us
  Pallas kernels  73.1 us (96%)
  local copies, waits for them, and re-layouts  1.84 us (2%)
    pallas_call x1, Pallas kernels, per_device(): pl.pallas_call(body, out_shape=jax.ShapeDtypeStruct((1, rows * shards, co...  73.1 us
    unnamed x1, local copies, waits for them, and re-layouts  1.84 us

profile of v7, /device:TPU:0, one launch (start us, length us, event | category | flops | bytes accessed | tf_op | source)
XLA Modules:
  0.0 75.6 jit_solution(12760028661652665288)
XLA Ops:
  0.7 73.1 %shard_map.55 = bf16[1,64,28672]{2,1,0:T(8,128)(2,1)S(1)} custom-call(f32[1,16,28672]{2,1,0:T(8,128)} %params_ref.1, f32[1,16,28672]{2,1,0:T(8,128)} %first_ref.1, f32[1,16,28672]{2,1,0:T(8,128)} %second_ref.1, bf16[4,1,16,28672]{3,2,1,0:T(8,128)(2,1)} %grads_ref.1, f32[1]{0:T(128)S(6)} %copy.7.weight_ref), custom_call_target="tpu_custom_call" | custom-call | tf_op jit(solution)/shard_map/pallas_call | solution.py:617
  73.7 1.8 %copy.8 = bf16[1,64,28672]{2,1,0:T(8,128)(2,1)} copy(bf16[1,64,28672]{2,1,0:T(8,128)(2,1)S(1)} %shard_map.55) | data formatting | bytes 7340032
